TPU v7x, 256 devices: a whole 4x4x8 slice. The times are simulated.
256 devices in a mesh: dp: 8 (over x, core), mp: 32 (over y, z).
Axes of the slice: x: 4, y: 4, z: 8, core: 2. Of those that a mesh axis runs over, the one named last changes fastest.
Arguments:
- gradients: bfloat16 [8, 4096, 16384], P('dp', None, 'mp'), may hold values from -40 to 40
- owner_table: int32 [512], replicated, may hold values from 0 to 31, as said below
Outputs:
- root_stacks: float32 [32, 24, 512, 512], P('mp', 'dp')
- slab_roots: float32 [16, 512, 16384], P(None, 'dp', 'mp')
Inputs may be any that keep to these rules, and one draw needn't show every extreme that they name: `owner_table`: statistic m * 16 + i belongs to column slab m. No owner is named by more than 24 statistics and some owner by exactly 24; among the 16 statistics of one column slab no owner is named more than 1 times, and some slab names some owner exactly 1 times.
All inputs are finite; a program needn't handle non-finite values.
Results may differ from a plain program's by a relative error of at most 0.0017.
Values may be sent and summed in bfloat16 or wider, within the bound.
No kernel may reach another device: no remote copies, remote signals or barrier semaphores. Data moves between devices by JAX's collectives and lax.ppermute only.
A program may use at most 320 MiB of HBM per device.

v0:
```python
import jax
import jax.numpy as jnp
from jax import lax
from jax.sharding import PartitionSpec as P

ITERS = 3
CAP = 24


def batched(first, second):
    return jnp.einsum("kab,kbc->kac", first, second, precision=lax.Precision.HIGHEST)


def newton_roots(statistics, iterations):
    matrix_size = statistics.shape[-1]
    identity = jnp.eye(matrix_size, dtype=jnp.float32)
    diagonal_mean = jnp.mean(jnp.diagonal(statistics, axis1=1, axis2=2), axis=1)
    damped = statistics + 0.1 * diagonal_mean[:, None, None] * identity[None]
    mean_square = jnp.mean(damped * damped, axis=(1, 2))
    norm_scale = matrix_size * jnp.sqrt(mean_square + 1e-06)
    matrix = damped / norm_scale[:, None, None]
    root_scale = norm_scale ** (-0.25)
    current = matrix
    for iteration in range(iterations):
        factor = (5.0 * identity - matrix) * 0.25
        if iteration == 0:
            current = factor * root_scale[:, None, None]
        else:
            current = batched(current, factor)
        if iteration + 1 < iterations:
            square = batched(factor, factor)
            matrix = batched(square, batched(square, matrix))
    return current


def pick_rows(source, match_table):
    labels = jnp.arange(match_table.shape[1], dtype=jnp.int32)
    pick_index = jnp.sum(match_table * labels[None, :], axis=1)
    is_valid = jnp.sum(match_table, axis=1).astype(jnp.float32)
    return jnp.take(source, pick_index, axis=0) * is_valid[:, None, None]


def make_plan(owner_table, model_index, model_count, per_slab, pair_count):
    stat_count = owner_table.shape[0]
    owner_ids = jnp.arange(model_count, dtype=jnp.int32)
    onehot = (owner_table[:, None] == owner_ids[None, :]).astype(jnp.int32)
    slot_number = jnp.sum((jnp.cumsum(onehot, axis=0) - onehot) * onehot, axis=1)
    owner_grid = onehot.reshape(model_count, per_slab, model_count)
    pair_rank = jnp.sum((jnp.cumsum(owner_grid, axis=1) - owner_grid) * owner_grid, axis=2).reshape(
        stat_count
    )
    stat_ids = jnp.arange(stat_count, dtype=jnp.int32)
    position = stat_ids // per_slab * pair_count + pair_rank
    owner_loads = jnp.sum(onehot, axis=0)
    first_stat = model_index * per_slab
    targets = lax.dynamic_slice_in_dim(owner_table * pair_count + pair_rank, first_stat, per_slab)
    slot_ids = jnp.arange(CAP, dtype=jnp.int32)
    slot_match = (
        (owner_table[None, :] == model_index) & (slot_number[None, :] == slot_ids[:, None])
    ).astype(jnp.int32)
    stack_index = jnp.sum(slot_match * position[None, :], axis=1)
    stack_valid = jnp.sum(slot_match, axis=1)
    return (targets, stack_index, stack_valid, owner_loads)


def to_owner(pieces, route_plan, model_count, pair_count):
    targets, stack_index, stack_valid, owner_loads = route_plan
    places = jnp.arange(model_count * pair_count, dtype=jnp.int32)
    send_match = (places[:, None] == targets[None, :]).astype(jnp.int32)
    incoming = lax.all_to_all(
        pick_rows(pieces, send_match), "mp", split_axis=0, concat_axis=0, tiled=True
    )
    slot_match = (stack_index[:, None] == places[None, :]).astype(jnp.int32) * stack_valid[:, None]
    slot_stack = pick_rows(incoming, slot_match)
    return lax.all_to_all(slot_stack, "dp", split_axis=0, concat_axis=1, tiled=True)


def row_sums(rounded, data_count):
    return lax.psum_scatter(
        rounded.astype(jnp.bfloat16), "dp", scatter_dimension=1, tiled=True
    ).astype(jnp.float32) * (1.0 / data_count)


def on_device(gradients, owner_table):
    data_count = lax.axis_size("dp")
    model_count = lax.axis_size("mp")
    model_index = lax.axis_index("mp")
    block_size = gradients.shape[2]
    row_blocks = gradients.shape[1] // block_size
    per_slab = 2 * row_blocks
    pair_count = (CAP + model_count - 1) // model_count
    local_blocks = gradients[0].reshape(row_blocks, block_size, block_size)
    left_gram = jnp.einsum(
        "rab,rcb->rac", local_blocks, local_blocks, preferred_element_type=jnp.float32
    )
    right_gram = jnp.einsum(
        "rab,rac->rbc", local_blocks, local_blocks, preferred_element_type=jnp.float32
    )
    partial_value = jnp.stack([left_gram, right_gram], axis=1).reshape(
        per_slab, block_size, block_size
    )
    rounded = lax.optimization_barrier(partial_value.astype(jnp.bfloat16)).astype(jnp.float32)
    route_plan = make_plan(owner_table, model_index, model_count, per_slab, pair_count)
    stat_sums = row_sums(rounded, data_count)
    whole_stats = lax.all_to_all(stat_sums, "dp", split_axis=0, concat_axis=1, tiled=True)
    home_roots = newton_roots(whole_stats, ITERS)
    slab_roots = lax.all_to_all(home_roots, "dp", split_axis=1, concat_axis=0, tiled=True)
    root_stacks = to_owner(slab_roots, route_plan, model_count, pair_count)
    return (root_stacks[None], slab_roots)


def solution(mesh):
    placed = (P("dp", None, "mp"), P())
    return jax.shard_map(
        on_device,
        mesh=mesh,
        in_specs=placed,
        out_specs=(P("mp", "dp", None, None), P(None, "dp", "mp")),
        check_vma=False,
    )
```

profile of v0, /device:TPU:1, one launch (start us, length us, event | category | flops | bytes accessed | tf_op | source)
XLA Modules:
  0.0 429.4 jit_solution(11550806026041133671)
XLA Ops:
  7.2 6.0 %convert_bitcast_fusion = bf16[8,1,512,512]{3,2,0,1:T(8,128)(2,1)S(1)} fusion(bf16[8,512,512]{2,1,0:T(8,128)(2,1)} %bitcast.68), kind=kOutput, calls=%fused_computation.5 | convolution fusion | flops 2149580800 | bytes 8388608 | tf_op jit(solution)/shard_map/rab,rac->rbc/dot_general | solution.py:96
  13.2 4.4 %convert_bitcast_fusion.1 = bf16[8,1,512,512]{3,2,0,1:T(8,128)(2,1)} fusion(bf16[8,512,512]{2,1,0:T(8,128)(2,1)S(1)} %bitcast.69), kind=kOutput, calls=%fused_computation.6 | convolution fusion | flops 2149580800 | bytes 8388608 | tf_op jit(solution)/shard_map/rab,rcb->rac/dot_general | solution.py:93
  17.6 6.2 %pad_maximum_fusion = bf16[8,2,512,512]{3,2,0,1:T(8,128)(2,1)} fusion(bf16[8,1,512,512]{3,2,0,1:T(8,128)(2,1)S(1)} %convert_bitcast_fusion, bf16[8,1,512,512]{3,2,0,1:T(8,128)(2,1)} %convert_bitcast_fusion.1), kind=kLoop, calls=%fused_computation.3 | loop fusion | flops 4194304 | bytes 16777216 | tf_op jit(solution)/shard_map/stack | solution.py:99
  23.7 7.3 %copy.30 = bf16[8,2,512,512]{3,2,1,0:T(8,128)(2,1)} copy(bf16[8,2,512,512]{3,2,0,1:T(8,128)(2,1)} %pad_maximum_fusion) | data formatting | bytes 16777216 | tf_op jit(solution)/shard_map/stack | solution.py:99
  31.1 58.4 %reduce-scatter.2.cloned.1.call-done = bf16[16,64,512]{2,1,0:T(8,128)(2,1)} async-done(((bf16[16,512,512]{2,1,0:T(8,128)(2,1)}), bf16[16,64,512]{2,1,0:T(8,128)(2,1)}) %reduce-scatter.2.cloned.1.call-update) | async-done | bytes 1048592 | tf_op jit(solution)/shard_map/reduce_scatter | solution.py:79
  89.5 2.8 convert_multiply_fusion
  92.3 4.7 %all-to-all-start = ((f32[16,64,512]{2,1,0:T(8,128)}), f32[16,64,512]{2,1,0:T(8,128)S(1)}, u32[]{:S(2)}, u32[]{:S(2)}) async-start(f32[16,64,512]{2,1,0:T(8,128)} %convert_multiply_fusion), calls=%async_computation.1 | async-start | bytes 4194304 | tf_op jit(solution)/shard_map/all_to_all | solution.py:105
  99.4 23.9 %all-to-all-done = f32[16,64,512]{2,1,0:T(8,128)S(1)} async-done(((f32[16,64,512]{2,1,0:T(8,128)}), f32[16,64,512]{2,1,0:T(8,128)S(1)}, u32[]{:S(2)}, u32[]{:S(2)}) %all-to-all-start) | async-done | bytes 2097184 | tf_op jit(solution)/shard_map/all_to_all | solution.py:105
  123.3 1.3 copy-done.1
  124.6 1.8 copy.31
  126.4 59.5 %copy.32 = f32[2,512,512]{0,2,1:T(8,128)} copy(f32[2,512,512]{2,1,0:T(8,128)S(1)} %bitcast.63) | data formatting | bytes 4194304 | tf_op jit(solution)/shard_map/all_to_all | solution.py:105
  185.9 5.7 %gather_fusion = f32[512,2]{1,0:T(8,128)S(1)} fusion(f32[2,512,512]{0,2,1:T(8,128)} %copy.32, s32[512]{0:T(512)S(1)} %bitcast.61), kind=kCustom, calls=%fused_computation | custom fusion | bytes 12288 | tf_op jit(solution)/shard_map/jit(diagonal)/gather | solution.py:17
  191.7 2.5 multiply_reduce_fusion
  194.7 3.7 fusion.3
  198.4 3.5 fusion.42
  201.9 3.5 fusion.43
  205.5 4.0 fusion.9
  209.4 3.5 fusion.44
  213.0 3.5 fusion.45
  216.5 3.7 fusion.5
  220.3 3.9 fusion
  224.2 2.9 copy.33
  227.1 4.6 %all-to-all-start.1 = ((f32[2,512,512]{2,0,1:T(2,128)}), f32[2,512,512]{2,0,1:T(2,128)S(1)}, u32[]{:S(2)}, u32[]{:S(2)}) async-start(f32[2,512,512]{2,0,1:T(2,128)} %copy.33), calls=%async_computation.2 | async-start | bytes 4194304 | tf_op jit(solution)/shard_map/all_to_all | solution.py:107
  232.8 25.1 %all-to-all-done.1 = f32[2,512,512]{2,0,1:T(2,128)S(1)} async-done(((f32[2,512,512]{2,0,1:T(2,128)}), f32[2,512,512]{2,0,1:T(2,128)S(1)}, u32[]{:S(2)}, u32[]{:S(2)}) %all-to-all-start.1) | async-done | bytes 2097184 | tf_op jit(solution)/shard_map/all_to_all | solution.py:107
  259.3 2.0 copy.34
  261.3 2.8 gather_fusion.1
  264.1 5.1 %select_multiply_fusion = f32[32,64,512]{2,1,0:T(8,128)} fusion(f32[32,64,512]{2,1,0:T(8,128)} %gather_fusion.1, f32[32]{0:T(128)S(1)} %convert_element_type.59, pred[32]{0:T(512)(128)(4,1)S(1)} %compare_and_fusion), kind=kLoop, calls=%fused_computation.4 | loop fusion | flops 2097152 | bytes 8388768 | tf_op jit(solution)/shard_map/mul | solution.py:40
  269.2 9.7 %all-to-all-start.2 = ((f32[32,64,512]{2,1,0:T(8,128)}), f32[32,64,512]{2,1,0:T(8,128)}, u32[]{:S(2)}, u32[]{:S(2)}) async-start(f32[32,64,512]{2,1,0:T(8,128)} %select_multiply_fusion), calls=%async_computation.3 | async-start | bytes 8388608 | tf_op jit(solution)/shard_map/all_to_all | solution.py:70
  280.8 90.8 %all-to-all-done.2 = f32[32,64,512]{2,1,0:T(8,128)} async-done(((f32[32,64,512]{2,1,0:T(8,128)}), f32[32,64,512]{2,1,0:T(8,128)}, u32[]{:S(2)}, u32[]{:S(2)}) %all-to-all-start.2) | async-done | bytes 4194336 | tf_op jit(solution)/shard_map/all_to_all | solution.py:70
  371.7 2.9 gather_fusion.2
  375.1 45.0 %all_to_all.56 = f32[24,64,512]{2,1,0:T(8,128)S(1)} all-to-all(f32[24,64,512]{2,1,0:T(8,128)S(1)} %select_multiply_fusion.1), channel_id=1, replica_groups=mesh['dp'=8,'mp'=32] {'dp'}, dimensions={0} | all-to-all | bytes 6291456 | tf_op jit(solution)/shard_map/all_to_all | solution.py:75
  420.2 2.0 copy.35
  (48 shorter events, 7.8 us)
Async XLA Ops:
  7.2 82.3 %reduce-scatter.2.cloned.1.call-start = ((), (), s32[]{:S(2)}) async-start(), calls=%async_computation.5 | async-start | bytes 9437184 | tf_op jit(solution)/shard_map/reduce_scatter | solution.py:79
  7.2 6.0 %copy-start.2 = (bf16[1,4096,512]{2,1,0:T(8,128)(2,1)S(1)}, bf16[1,4096,512]{2,1,0:T(8,128)(2,1)}, u32[]{:S(2)}) copy-start(bf16[1,4096,512]{2,1,0:T(8,128)(2,1)} %param.2) | copy-start | bytes 12582916
  92.3 30.9 %all-to-all-start = ((f32[16,64,512]{2,1,0:T(8,128)}), f32[16,64,512]{2,1,0:T(8,128)S(1)}, u32[]{:S(2)}, u32[]{:S(2)}) async-start(f32[16,64,512]{2,1,0:T(8,128)} %convert_multiply_fusion), calls=%async_computation.1 | async-start | bytes 4194304 | tf_op jit(solution)/shard_map/all_to_all | solution.py:105
  123.3 1.3 copy-start.1
  191.7 2.5 copy-start.4
  227.1 4.6 %copy-start.5 = (s32[512]{0:T(512)S(1)}, s32[512]{0:T(512)}, u32[]{:S(2)}) copy-start(s32[512]{0:T(512)} %param.3) | copy-start | bytes 6148
  227.1 30.8 %all-to-all-start.1 = ((f32[2,512,512]{2,0,1:T(2,128)}), f32[2,512,512]{2,0,1:T(2,128)S(1)}, u32[]{:S(2)}, u32[]{:S(2)}) async-start(f32[2,512,512]{2,0,1:T(2,128)} %copy.33), calls=%async_computation.2 | async-start | bytes 4194304 | tf_op jit(solution)/shard_map/all_to_all | solution.py:107
  258.0 1.3 copy-start.3
  261.3 2.8 copy-start
  269.2 102.5 %all-to-all-start.2 = ((f32[32,64,512]{2,1,0:T(8,128)}), f32[32,64,512]{2,1,0:T(8,128)}, u32[]{:S(2)}, u32[]{:S(2)}) async-start(f32[32,64,512]{2,1,0:T(8,128)} %select_multiply_fusion), calls=%async_computation.3 | async-start | bytes 8388608 | tf_op jit(solution)/shard_map/all_to_all | solution.py:70
Sparse Core Ops, SparseCore 0:
  31.2 58.2 reduce-scatter.1
where the time goes:
time: 435 us; the launch traced here: 429 us
  waiting for transfers between devices  198 us (46%)
  local copies, waits for them, and re-layouts  90.2 us (21%)
  blocking collectives  45 us (10%)
  matrix products  39.8 us (9%)
  other arithmetic  22.4 us (5%)
  starting transfers between devices  19 us (4%)
  between operations  14.7 us (3%)
    all_to_all x1, waiting for transfers between devices, to_owner(): lax.all_to_all(pick_rows(pieces, send_match), 'mp', split_axis=0, concat_...  90.8 us
    all_to_all x2, local copies, waits for them, and re-layouts, on_device(): lax.all_to_all(stat_sums, 'dp', split_axis=0, concat_axis=1, tiled=True)  61.3 us
    reduce_scatter x1, waiting for transfers between devices, row_sums(): lax.psum_scatter(rounded.astype(jnp.bfloat16), 'dp', scatter_dimension=1,...  58.4 us
    all_to_all x1, blocking collectives, to_owner(): lax.all_to_all(slot_stack, 'dp', split_axis=0, concat_axis=1, tiled=True)  45 us
    dot_general x8, matrix products, batched(): jnp.einsum('kab,kbc->kac', first, second, precision=lax.Precision.HIGHEST)  29.5 us
    all_to_all x1, waiting for transfers between devices, on_device(): lax.all_to_all(home_roots, 'dp', split_axis=1, concat_axis=0, tiled=True)  25.1 us
    all_to_all x1, waiting for transfers between devices, on_device(): lax.all_to_all(stat_sums, 'dp', split_axis=0, concat_axis=1, tiled=True)  23.9 us
    all_to_all x1, starting transfers between devices, to_owner(): lax.all_to_all(pick_rows(pieces, send_match), 'mp', split_axis=0, concat_...  9.71 us
  transfers between devices with their start and end apart: 4, of which 4 were waited for; matrix products, arithmetic and copies ran while one was open for 1% of the time, Pallas kernels for 0%

commit v1 on v0

v1 whole, which is shorter than its diff:
```python
import functools

import jax
import jax.numpy as jnp
from jax import lax
from jax.experimental import pallas as pl
from jax.experimental.pallas import tpu as pltpu
from jax.sharding import PartitionSpec as P

CAP = 24
BLOCK = 512
TILE = 128
UPPER = [(0, 0), (0, 1), (0, 2), (0, 3), (1, 1), (1, 2), (1, 3), (2, 2), (2, 3), (3, 3)]
HALF = len(UPPER) // 2
HALF_ROWS = HALF * TILE
PACKED_ROWS = len(UPPER) * TILE
ALPHA_ORDER = (1, 2, 0, 3)
BETA_ORDER = (3, 2, 0, 1)
INTERPRET = False
F32 = jnp.float32
BF16 = jnp.bfloat16


def rows_of(block):
    return slice(block * TILE, (block + 1) * TILE)


def dot(first, second, dims=((1,), (0,))):
    return lax.dot_general(first, second, (dims, ((), ())), preferred_element_type=F32)


def gram_kernel(place_ref, block_ref, alpha_ref, beta_ref):
    block = block_ref[0]
    half = BLOCK // 2
    for side in range(2):
        dims = ((1,), (1,)) if side == 0 else ((0,), (0,))
        low = block[:half] if side == 0 else block[:, :half]
        high = block[half:] if side == 0 else block[:, half:]
        top = dot(low, block, dims).astype(BF16)
        bottom = dot(high, high, dims).astype(BF16)
        for index, (row, column) in enumerate(UPPER):
            if row < 2:
                piece = top[rows_of(row), rows_of(column)]
            else:
                piece = bottom[rows_of(row - 2), rows_of(column - 2)]
            target = alpha_ref if index < HALF else beta_ref
            target[0, side, rows_of(index % HALF), :] = piece


def gram_blocks(blocks, place, core_bit):
    def which(order):
        def index_map(step, place_ref):
            return (order(step), 0, 0, 0)

        return index_map

    alpha_slot = [ALPHA_ORDER.index(t) for t in range(4)]
    beta_slot = [BETA_ORDER.index(t) for t in range(4)]

    def table(slots):
        def order(step):
            result = slots[3]
            for t in range(3):
                result = jnp.where(step == t, slots[t], result)
            return result

        return order

    shape = jax.ShapeDtypeStruct((4, 2, HALF_ROWS, TILE), BF16)
    grid_spec = pltpu.PrefetchScalarGridSpec(
        num_scalar_prefetch=1,
        grid=(4,),
        in_specs=[
            pl.BlockSpec(
                (1, BLOCK, BLOCK),
                lambda step, place_ref: (place_ref[0] ^ (2 * step + core_bit), 0, 0),
            )
        ],
        out_specs=[
            pl.BlockSpec((1, 2, HALF_ROWS, TILE), which(table(alpha_slot))),
            pl.BlockSpec((1, 2, HALF_ROWS, TILE), which(table(beta_slot))),
        ],
    )
    return pl.pallas_call(
        gram_kernel,
        out_shape=(shape, shape),
        grid_spec=grid_spec,
        interpret=INTERPRET,
        name="gram" + str(core_bit),
        cost_estimate=pl.CostEstimate(
            flops=4 * 2 * 3 * BLOCK**3 // 2, bytes_accessed=5 * 2**20, transcendentals=0
        ),
    )(place, blocks)


def iota(shape, axis):
    return lax.broadcasted_iota(jnp.int32, shape, axis)


def total(value):
    return jnp.sum(jnp.sum(value, axis=0, keepdims=True), axis=1, keepdims=True)


def power_four(matrix, small, product):
    square = dot(small, small)
    part = (square * 0.0625 - 0.625 * matrix).astype(BF16)
    once = 1.5625 * matrix + dot(part, small)
    return 1.5625 * once + dot(part, once.astype(BF16))


def newton_kernel(parts, data_count, refs, rows_ref, packed_ref, stat_ref):
    row_ids = iota((BLOCK, BLOCK), 0)
    column_ids = iota((BLOCK, BLOCK), 1)
    on_diagonal = row_ids == column_ids
    spare = (row_ids % 64 == 1) & (column_ids == row_ids - 1)
    for stat in range(2):
        for index, (row, column) in enumerate(UPPER):
            piece = None
            for ref in refs[parts * (index // HALF) : parts * (index // HALF) + parts]:
                term = ref[0, stat, rows_of(index % HALF), :].astype(F32)
                piece = term if piece is None else piece + term
            stat_ref[rows_of(row), rows_of(column)] = piece
            if row != column:
                stat_ref[rows_of(column), rows_of(row)] = piece.T
        statistic = stat_ref[...] * (1.0 / data_count)
        diagonal_mean = total(jnp.where(on_diagonal, statistic, 0.0)) * (1.0 / BLOCK)
        damped = statistic + jnp.where(on_diagonal, 0.1 * diagonal_mean, 0.0)
        mean_square = total(damped * damped) * (1.0 / BLOCK**2)
        norm_scale = BLOCK * jnp.sqrt(mean_square + 1e-06)
        root_scale = lax.rsqrt(jnp.sqrt(norm_scale))
        first = damped / norm_scale
        first_small = first.astype(BF16)
        second = power_four(first, first_small, None)
        second_small = second.astype(BF16)
        pair = dot(first_small, second_small) * 0.0625 - 0.3125 * (first + second)
        third = power_four(second, second_small, None)
        rest = 1.25 * pair - 0.390625 * third - 0.25 * dot(pair.astype(BF16), third.astype(BF16))
        rest = rest * root_scale
        rest_mean = total(jnp.where(on_diagonal, rest, 0.0)) * (1.0 / BLOCK)
        identity_part = 1.953125 * root_scale
        center = (identity_part + rest_mean).astype(BF16).astype(F32)
        rest = rest + jnp.where(on_diagonal, identity_part - center, 0.0)
        sent = jnp.where(spare, center, rest).astype(BF16)
        for device in range(8):
            rows_ref[device, stat] = sent[device * 64 : (device + 1) * 64]
        for index, (row, column) in enumerate(UPPER):
            piece = sent[rows_of(row), rows_of(column)]
            start = index * TILE
            while start < (index + 1) * TILE:
                device = start // CHUNK
                stop = min((index + 1) * TILE, (device + 1) * CHUNK)
                packed_ref[device, stat, start - device * CHUNK : stop - device * CHUNK, :] = piece[
                    start - index * TILE : stop - index * TILE
                ]
                start = stop


CHUNK = PACKED_ROWS // 8


def newton(alpha, beta, data_count):
    parts = len(alpha)

    def body(*refs):
        newton_kernel(parts, data_count, refs[: 2 * parts], *refs[2 * parts :])

    def spec(place):
        return pl.BlockSpec((1, 2, HALF_ROWS, TILE), lambda step: (place, 0, 0, 0))

    return pl.pallas_call(
        body,
        grid=(1,),
        in_specs=[spec(place) for _, place in alpha + beta],
        out_specs=[
            pl.BlockSpec((8, 2, 64, BLOCK), lambda step: (0, 0, 0, 0)),
            pl.BlockSpec((8, 2, CHUNK, TILE), lambda step: (0, 0, 0, 0)),
        ],
        out_shape=(
            jax.ShapeDtypeStruct((8, 2, 64, BLOCK), BF16),
            jax.ShapeDtypeStruct((8, 2, CHUNK, TILE), BF16),
        ),
        scratch_shapes=[pltpu.VMEM((BLOCK, BLOCK), F32)],
        interpret=INTERPRET,
        name="newton",
        cost_estimate=pl.CostEstimate(
            flops=2 * 8 * 2 * BLOCK**3, bytes_accessed=6 * 2**20, transcendentals=0
        ),
    )(*[array for array, _ in alpha + beta])


def pick_kernel(index_ref, source_ref, out_ref):
    def step(place, carry):
        out_ref[place] = source_ref[index_ref[place]]
        return carry

    lax.fori_loop(0, out_ref.shape[0], step, 0)


def pick(source, index, name):
    count = index.shape[0]
    return pl.pallas_call(
        pick_kernel,
        out_shape=jax.ShapeDtypeStruct((count,) + source.shape[1:], source.dtype),
        in_specs=[
            pl.BlockSpec(memory_space=pltpu.SMEM),
            pl.BlockSpec(memory_space=pltpu.VMEM),
        ],
        out_specs=pl.BlockSpec(memory_space=pltpu.VMEM),
        interpret=INTERPRET,
        name=name,
        cost_estimate=pl.CostEstimate(flops=2 * 10**6, bytes_accessed=2 * 2**20, transcendentals=0),
    )(index, source)


def make_plan(owner_table, model_index, model_count, per_slab):
    owner_ids = jnp.arange(model_count, dtype=jnp.int32)
    mine = lax.dynamic_slice_in_dim(owner_table, model_index * per_slab, per_slab)
    local_ids = jnp.arange(per_slab, dtype=jnp.int32)
    send_index = jnp.sum(
        jnp.where(mine[None, :] == owner_ids[:, None], local_ids[None, :], 0), axis=1
    )
    named = jnp.sum(
        (owner_table.reshape(model_count, per_slab) == model_index).astype(jnp.int32), axis=1
    )
    rank = jnp.sum(
        jnp.where(owner_ids[None, :] < owner_ids[:, None], named[None, :], 0), axis=1
    )
    slot_ids = jnp.arange(CAP, dtype=jnp.int32)
    match = (rank[None, :] == slot_ids[:, None]) & (named[None, :] > 0)
    slot_index = jnp.sum(jnp.where(match, owner_ids[None, :], 0), axis=1)
    return send_index, slot_index, jnp.sum(named)


def unpack_kernel(valid_ref, source_ref, out_ref, stack_ref):
    slot = pl.program_id(0)
    keep = valid_ref[slot] > 0

    @pl.when(keep)
    def _():
        for device in range(8):
            stack_ref[device * CHUNK : (device + 1) * CHUNK, :] = source_ref[device, 0].astype(F32)
        center = stack_ref[1:2, 0:1]
        row_ids = iota((TILE, TILE), 0)
        column_ids = iota((TILE, TILE), 1)
        spare = (row_ids % 64 == 1) & (column_ids == row_ids - 1)
        for index, (row, column) in enumerate(UPPER):
            piece = stack_ref[rows_of(index), :]
            if row == column:
                piece = jnp.where(spare, piece.T, piece)
                piece = jnp.where(row_ids == column_ids, piece + center, piece)
            else:
                out_ref[0, rows_of(column), rows_of(row)] = piece.T
            out_ref[0, rows_of(row), rows_of(column)] = piece

    @pl.when(jnp.logical_not(keep))
    def _():
        out_ref[...] = jnp.zeros_like(out_ref)


def unpack(source, valid):
    slots = source.shape[1]
    return pl.pallas_call(
        unpack_kernel,
        out_shape=jax.ShapeDtypeStruct((slots, BLOCK, BLOCK), F32),
        grid_spec=pltpu.PrefetchScalarGridSpec(
            num_scalar_prefetch=1,
            grid=(slots,),
            in_specs=[pl.BlockSpec((8, 1, CHUNK, TILE), lambda slot, valid_ref: (0, slot, 0, 0))],
            out_specs=pl.BlockSpec((1, BLOCK, BLOCK), lambda slot, valid_ref: (slot, 0, 0)),
            scratch_shapes=[pltpu.VMEM((PACKED_ROWS, TILE), F32)],
        ),
        interpret=INTERPRET,
        name="unpack",
        cost_estimate=pl.CostEstimate(flops=2 * 10**6, bytes_accessed=4 * 2**20, transcendentals=0),
    )(valid, source)


def finish_rows(rows, data_index):
    stats, count, width = rows.shape
    first = data_index * count
    columns = jnp.arange(width, dtype=jnp.int32)
    center = jnp.sum(jnp.where(columns == first, rows[:, 1, :].astype(F32), 0.0), axis=1)
    mirrored = jnp.sum(jnp.where(columns == first + 1, rows[:, 0, :].astype(F32), 0.0), axis=1)
    row_ids = iota((count, width), 0)
    column_ids = iota((count, width), 1) - first
    spare = (row_ids == 1) & (column_ids == 0)
    value = jnp.where(spare[None], mirrored[:, None, None], rows.astype(F32))
    return value + jnp.where((row_ids == column_ids)[None], center[:, None, None], 0.0)


def add(first, second):
    return (first.astype(F32) + second.astype(F32)).astype(BF16)


def exchange(value, bits, data_count):
    return lax.ppermute(value, "dp", [(d, d ^ bits) for d in range(data_count)])


def on_device(gradients, owner_table):
    data_count = lax.axis_size("dp")
    model_count = lax.axis_size("mp")
    data_index = lax.axis_index("dp")
    model_index = lax.axis_index("mp")
    row_blocks = gradients.shape[1] // BLOCK
    per_slab = 2 * row_blocks
    blocks = gradients[0].reshape(row_blocks, BLOCK, BLOCK)
    place = data_index.astype(jnp.int32).reshape(1)

    away_alpha, away_beta = gram_blocks(blocks, place, 1)
    got_alpha = exchange(away_alpha, 1, data_count)
    got_beta = exchange(away_beta, 1, data_count)
    own_alpha, own_beta = gram_blocks(blocks, place, 0)

    step_alpha = exchange(add(own_alpha[:2], got_alpha[:2]), 2, data_count)
    step_beta = exchange(add(own_beta[:2], got_beta[:2]), 6, data_count)

    def second(own, got, step, bits):
        value = own[3:4].astype(F32) + got[3:4].astype(F32) + step[1:2].astype(F32)
        return exchange(value.astype(BF16), bits, data_count)

    last_alpha = second(own_alpha, got_alpha, step_alpha, 6)
    last_beta = second(own_beta, got_beta, step_beta, 2)

    rows, packed = newton(
        [(own_alpha, 2), (got_alpha, 2), (step_alpha, 0), (last_alpha, 0)],
        [(own_beta, 2), (got_beta, 2), (step_beta, 0), (last_beta, 0)],
        data_count,
    )

    send_index, slot_index, load = make_plan(owner_table, model_index, model_count, per_slab)

    pieces = lax.all_to_all(packed, "dp", split_axis=0, concat_axis=0, tiled=True)
    row_pieces = lax.all_to_all(rows, "dp", split_axis=0, concat_axis=0, tiled=True)
    outgoing = pick(pieces.reshape(per_slab, CHUNK, TILE), send_index, "send_pick")
    incoming = lax.all_to_all(outgoing, "mp", split_axis=0, concat_axis=0, tiled=True)
    slab_roots = finish_rows(row_pieces.reshape(per_slab, BLOCK // data_count, BLOCK), data_index)
    slots = pick(incoming, slot_index, "slot_pick")
    stacked = lax.all_to_all(slots, "dp", split_axis=0, concat_axis=0, tiled=True)
    own_slots = CAP // data_count
    slot_ids = data_index * own_slots + jnp.arange(own_slots, dtype=jnp.int32)
    valid = (slot_ids < load).astype(jnp.int32)
    root_stacks = unpack(stacked.reshape(data_count, own_slots, CHUNK, TILE), valid)
    return (root_stacks[None], slab_roots)


def solution(mesh):
    placed = (P("dp", None, "mp"), P())
    return jax.shard_map(
        on_device,
        mesh=mesh,
        in_specs=placed,
        out_specs=(P("mp", "dp", None, None), P(None, "dp", "mp")),
        check_vma=False,
    )
```

time: 435 us -> 161 us (0.37); the launches traced: 429 us -> 160 us
  waiting for transfers between devices: 198 us -> 87.6 us
  local copies, waits for them, and re-layouts: 90.2 us -> 2.69 us
  blocking collectives: 45 us -> 0 us
  matrix products: 39.8 us -> 0 us
  Pallas kernels: 0 us -> 28 us
  between operations: 14.7 us -> 0.78 us
  starting transfers between devices: 19 us -> 32.6 us
  other arithmetic: 22.4 us -> 8.86 us
    all_to_all x3 -> x4, waiting for transfers between devices: 140 us -> 63.3 us  [the longest x1 30.7 us: on_device(): lax.all_to_all(outgoing, 'mp', split_axis=0, concat_axis=0, tiled=True)]
    all_to_all x4 -> x0, local copies, waits for them, and re-layouts: 65.2 us -> none  [the longest x2 61.3 us: on_device(): lax.all_to_all(stat_sums, 'dp', split_axis=0, concat_axis=1, tiled=True)]
    reduce_scatter x1 -> x0, waiting for transfers between devices: 58.4 us -> none  [row_sums(): lax.psum_scatter(rounded.astype(jnp.bfloat16), 'dp', scatter_dimension=1,...]
    all_to_all x1 -> x0, blocking collectives: 45 us -> none  [to_owner(): lax.all_to_all(slot_stack, 'dp', split_axis=0, concat_axis=1, tiled=True)]
    dot_general x10 -> x0, matrix products: 39.8 us -> none  [the longest x8 29.5 us: batched(): jnp.einsum('kab,kbc->kac', first, second, precision=lax.Precision.HIGHEST)]
    pallas_call x0 -> x6, Pallas kernels: none -> 28 us  [the longest x2 10 us: gram_blocks(): pl.pallas_call(gram_kernel, out_shape=(shape, shape), grid_spec=grid_spec...]
    ppermute x0 -> x6, waiting for transfers between devices: none -> 24.2 us  [exchange(): return lax.ppermute(value, 'dp', [(d, d ^ bits) for d in range(data_count)])]
    gather x3 -> x0, local copies, waits for them, and re-layouts: 11.4 us -> none  [the longest x2 5.72 us: pick_rows(): return jnp.take(source, pick_index, axis=0) * is_valid[:, None, None]]
  transfers between devices with their start and end apart: 4 -> 10, of which waited for: 4 -> 7; matrix products, arithmetic and copies ran while one was open for 1% -> 6% of each run, Pallas kernels for 0% -> 5%
where the time goes in v1:
time: 161 us; the launch traced here: 160 us
  waiting for transfers between devices  87.6 us (54%)
  starting transfers between devices  32.6 us (20%)
  Pallas kernels  28 us (17%)
  other arithmetic  8.86 us (6%)
  local copies, waits for them, and re-layouts  2.69 us (2%)
    all_to_all x1, waiting for transfers between devices, on_device(): lax.all_to_all(outgoing, 'mp', split_axis=0, concat_axis=0, tiled=True)  30.7 us
    ppermute x6, waiting for transfers between devices, exchange(): return lax.ppermute(value, 'dp', [(d, d ^ bits) for d in range(data_count)])  24.2 us
    all_to_all x1, waiting for transfers between devices, on_device(): lax.all_to_all(slots, 'dp', split_axis=0, concat_axis=0, tiled=True)  12.3 us
    all_to_all x1, waiting for transfers between devices, on_device(): lax.all_to_all(rows, 'dp', split_axis=0, concat_axis=0, tiled=True)  10.3 us
    all_to_all x1, waiting for transfers between devices, on_device(): lax.all_to_all(packed, 'dp', split_axis=0, concat_axis=0, tiled=True)  10.1 us
    all_to_all x1, starting transfers between devices, on_device(): lax.all_to_all(outgoing, 'mp', split_axis=0, concat_axis=0, tiled=True)  10.1 us
    pallas_call x2, Pallas kernels, gram_blocks(): pl.pallas_call(gram_kernel, out_shape=(shape, shape), grid_spec=grid_spec...  10 us
    pallas_call x1, Pallas kernels, newton(): pl.pallas_call(body, grid=(1,), in_specs=[spec(place) for _, place in alp...  8.93 us
  transfers between devices with their start and end apart: 10, of which 7 were waited for; matrix products, arithmetic and copies ran while one was open for 6% of the time, Pallas kernels for 5%

profile of v1, /device:TPU:1, one launch (start us, length us, event | category | flops | bytes accessed | tf_op | source)
XLA Modules:
  0.0 160.5 jit_solution(7920491733917850300)
XLA Ops:
  0.6 5.0 %gram1.1 = (bf16[4,2,640,128]{3,2,1,0:T(8,128)(2,1)}, bf16[4,2,640,128]{3,2,1,0:T(8,128)(2,1)}) custom-call(s32[1]{0:T(128)} %bitcast.place_ref, bf16[8,512,512]{2,1,0:T(8,128)(2,1)} %bitcast.20), custom_call_target="tpu_custom_call" | custom-call | flops 1610612736 | bytes 5242880 | tf_op jit(solution)/shard_map/gram1/pallas_call | solution.py:84
  5.7 3.2 %collective-permute-start.3 = (bf16[4,2,640,128]{3,2,1,0:T(8,128)(2,1)}, bf16[4,2,640,128]{3,2,1,0:T(8,128)(2,1)S(1)}, u32[]{:S(2)}, u32[]{:S(2)}) collective-permute-start(bf16[4,2,640,128]{3,2,1,0:T(8,128)(2,1)} %get-tuple-element.11), channel_id=1, source_target_pairs={{0,32},{32,0},{64,96},{96,64},{128,160},{160,128},{192,224},{224,1... | collective-permute-start | bytes 3932168 | tf_op jit(solution)/shard_map/ppermute | solution.py:296
  8.9 5.0 %gram0.1 = (bf16[4,2,640,128]{3,2,1,0:T(8,128)(2,1)}, bf16[4,2,640,128]{3,2,1,0:T(8,128)(2,1)}) custom-call(s32[1]{0:T(128)} %bitcast.place_ref, bf16[8,512,512]{2,1,0:T(8,128)(2,1)} %bitcast.21), custom_call_target="tpu_custom_call" | custom-call | flops 1610612736 | bytes 5242880 | tf_op jit(solution)/shard_map/gram0/pallas_call | solution.py:84
  13.9 1.8 %add_convert_fusion = bf16[2,2,640,128]{3,2,1,0:T(8,128)(2,1)S(1)} fusion(bf16[4,2,640,128]{3,2,1,0:T(8,128)(2,1)S(1)} %collective-permute-done.3.refs_5_, bf16[4,2,640,128]{3,2,1,0:T(8,128)(2,1)} %get-tuple-element.10.refs_4_), kind=kLoop, calls=%fused_computation.1 | loop fusion | flops 1310720 | bytes 1966080 | tf_op jit(solution)/shard_map/convert_element_type | solution.py:292
  15.6 0.9 collective-permute-start.4
  16.5 0.2 add_convert_fusion.1
  16.8 15.9 %collective-permute-done.4.refs_6_ = bf16[2,2,640,128]{3,2,1,0:T(8,128)(2,1)S(1)} collective-permute-done((bf16[2,2,640,128]{3,2,1,0:T(8,128)(2,1)S(1)}, bf16[2,2,640,128]{3,2,1,0:T(8,128)(2,1)S(1)}, u32[]{:S(2)}, u32[]{:S(2)}) %collective-permute-start.4) | collective-permute-done | bytes 655392 | tf_op jit(solution)/shard_map/ppermute | solution.py:296
  32.7 1.3 add_convert_fusion.2
  34.2 0.1 add_convert_fusion.3
  34.3 0.9 collective-permute-start.2
  35.2 6.8 %collective-permute-done.5.refs_7_ = bf16[1,2,640,128]{3,2,1,0:T(8,128)(2,1)S(1)} collective-permute-done((bf16[1,2,640,128]{3,2,1,0:T(8,128)(2,1)S(1)}, bf16[1,2,640,128]{3,2,1,0:T(8,128)(2,1)S(1)}, u32[]{:S(2)}, u32[]{:S(2)}) %collective-permute-start.5) | collective-permute-done | bytes 327712 | tf_op jit(solution)/shard_map/ppermute | solution.py:296
  42.0 1.5 collective-permute-done.2.refs_3_
  43.5 0.7 copy-done.10
  44.2 8.9 %newton.1 = (bf16[8,2,64,512]{3,2,1,0:T(8,128)(2,1)}, bf16[8,2,160,128]{3,2,1,0:T(8,128)(2,1)}) custom-call(bf16[4,2,640,128]{3,2,1,0:T(8,128)(2,1)} %get-tuple-element.8.refs_0_, bf16[4,2,640,128]{3,2,1,0:T(8,128)(2,1)} %copy-done.4, bf16[2,2,640,128]{3,2,1,0:T(8,128)(2,1)} %copy-done.7, bf16[1,2,640,128]{3,2,1,0:T(8,128)(2,1)} %copy-done.10, ...), custom_call_target="tpu_custom_call" | custom-call | flops 4294967296 | bytes 6291456 | tf_op jit(solution)/shard_map/newton/pallas_call | solution.py:170
  53.2 5.8 %all-to-all-start = ((bf16[8,2,160,128]{3,2,1,0:T(8,128)(2,1)}), bf16[8,2,160,128]{3,2,1,0:T(8,128)(2,1)S(1)}, u32[]{:S(2)}, u32[]{:S(2)}) async-start(bf16[8,2,160,128]{3,2,1,0:T(8,128)(2,1)} %get-tuple-element.12), calls=%async_computation | async-start | bytes 1310720 | tf_op jit(solution)/shard_map/all_to_all | solution.py:332
  59.0 0.6 select_reduce_fusion.2.index_ref
  59.7 10.1 %all-to-all-done = bf16[8,2,160,128]{3,2,1,0:T(8,128)(2,1)S(1)} async-done(((bf16[8,2,160,128]{3,2,1,0:T(8,128)(2,1)}), bf16[8,2,160,128]{3,2,1,0:T(8,128)(2,1)S(1)}, u32[]{:S(2)}, u32[]{:S(2)}) %all-to-all-start) | async-done | bytes 655392 | tf_op jit(solution)/shard_map/all_to_all | solution.py:332
  69.8 0.8 copy-done.2
  70.6 2.4 %send_pick.1 = bf16[32,160,128]{2,1,0:T(8,128)(2,1)} custom-call(s32[32]{0:T(128)} %select_reduce_fusion.2.index_ref, bf16[16,160,128]{2,1,0:T(8,128)(2,1)} %bitcast.19), custom_call_target="tpu_custom_call" | custom-call | flops 2000000 | bytes 2097152 | tf_op jit(solution)/shard_map/send_pick/pallas_call | solution.py:201
  73.0 10.1 %all-to-all-start.1 = ((bf16[32,160,128]{2,1,0:T(8,128)(2,1)}), bf16[32,160,128]{2,1,0:T(8,128)(2,1)S(1)}, u32[]{:S(2)}, u32[]{:S(2)}) async-start(bf16[32,160,128]{2,1,0:T(8,128)(2,1)} %send_pick.1), calls=%async_computation.1 | async-start | bytes 2621440 | tf_op jit(solution)/shard_map/all_to_all | solution.py:335
  83.1 0.6 fusion.3
  83.7 30.7 %all-to-all-done.1.source_ref = bf16[32,160,128]{2,1,0:T(8,128)(2,1)S(1)} async-done(((bf16[32,160,128]{2,1,0:T(8,128)(2,1)}), bf16[32,160,128]{2,1,0:T(8,128)(2,1)S(1)}, u32[]{:S(2)}, u32[]{:S(2)}) %all-to-all-start.1) | async-done | bytes 1310752 | tf_op jit(solution)/shard_map/all_to_all | solution.py:335
  114.5 7.1 %all-to-all-start.3 = ((bf16[8,2,64,512]{3,2,1,0:T(8,128)(2,1)}), bf16[8,2,64,512]{3,2,1,0:T(8,128)(2,1)S(1)}, u32[]{:S(2)}, u32[]{:S(2)}) async-start(bf16[8,2,64,512]{3,2,1,0:T(8,128)(2,1)} %get-tuple-element.13), calls=%async_computation.3 | async-start | bytes 2097152 | tf_op jit(solution)/shard_map/all_to_all | solution.py:333
  121.8 1.2 compare_convert_fusion.valid_ref
  123.2 0.7 select_reduce_fusion.1.index_ref
  123.9 2.5 %slot_pick.1 = bf16[24,160,128]{2,1,0:T(8,128)(2,1)} custom-call(s32[24]{0:T(128)} %select_reduce_fusion.1.index_ref, bf16[32,160,128]{2,1,0:T(8,128)(2,1)} %copy-done), custom_call_target="tpu_custom_call" | custom-call | flops 2000000 | bytes 2097152 | tf_op jit(solution)/shard_map/slot_pick/pallas_call | solution.py:201
  126.3 10.3 %all-to-all-done.3 = bf16[8,2,64,512]{3,2,1,0:T(8,128)(2,1)S(1)} async-done(((bf16[8,2,64,512]{3,2,1,0:T(8,128)(2,1)}), bf16[8,2,64,512]{3,2,1,0:T(8,128)(2,1)S(1)}, u32[]{:S(2)}, u32[]{:S(2)}) %all-to-all-start.3) | async-done | bytes 1048608 | tf_op jit(solution)/shard_map/all_to_all | solution.py:333
  136.6 4.4 %all-to-all-start.2 = ((bf16[24,160,128]{2,1,0:T(8,128)(2,1)}), bf16[24,160,128]{2,1,0:T(8,128)(2,1)S(1)}, u32[]{:S(2)}, u32[]{:S(2)}) async-start(bf16[24,160,128]{2,1,0:T(8,128)(2,1)} %slot_pick.1), calls=%async_computation.2 | async-start | bytes 1966080 | tf_op jit(solution)/shard_map/all_to_all | solution.py:338
  141.3 1.8 %select_add_fusion = f32[16,64,512]{2,1,0:T(8,128)} fusion(f32[16]{0:T(128)S(1)} %get-tuple-element.18, f32[16]{0:T(128)S(1)} %get-tuple-element.19, pred[64,512]{1,0:T(8,128)(4,1)S(1)} %get-tuple-element.20, pred[64,512]{1,0:T(8,128)(4,1)S(1)} %get-tuple-element.21, bf16[8,2,64,512]{3,2,1,0:T(8,128)(2,1)S(1)} %all-to-all-done.3), kind=kLoop, calls=%fused_computation | loop fusion | flops 2097152 | bytes 3211392 | tf_op jit(solution)/shard_map/add | solution.py:288
  143.1 12.3 %all-to-all-done.2 = bf16[24,160,128]{2,1,0:T(8,128)(2,1)S(1)} async-done(((bf16[24,160,128]{2,1,0:T(8,128)(2,1)}), bf16[24,160,128]{2,1,0:T(8,128)(2,1)S(1)}, u32[]{:S(2)}, u32[]{:S(2)}) %all-to-all-start.2) | async-done | bytes 983072 | tf_op jit(solution)/shard_map/all_to_all | solution.py:338
  155.3 0.9 copy-done.1
  156.3 4.2 %unpack.1 = f32[3,512,512]{2,1,0:T(8,128)} custom-call(s32[3]{0:T(128)} %compare_convert_fusion.valid_ref, bf16[8,3,160,128]{3,2,1,0:T(8,128)(2,1)} %bitcast.17), custom_call_target="tpu_custom_call" | custom-call | flops 2000000 | bytes 4194304 | tf_op jit(solution)/shard_map/unpack/pallas_call | solution.py:262
  (38 shorter events, 0.9 us)
Async XLA Ops:
  5.7 8.2 %collective-permute-start.3 = (bf16[4,2,640,128]{3,2,1,0:T(8,128)(2,1)}, bf16[4,2,640,128]{3,2,1,0:T(8,128)(2,1)S(1)}, u32[]{:S(2)}, u32[]{:S(2)}) collective-permute-start(bf16[4,2,640,128]{3,2,1,0:T(8,128)(2,1)} %get-tuple-element.11), channel_id=1, source_target_pairs={{0,32},{32,0},{64,96},{96,64},{128,160},{160,128},{192,224},{224,1... | collective-permute-start | bytes 3932168 | tf_op jit(solution)/shard_map/ppermute | solution.py:296
  8.9 7.6 %collective-permute-start = (bf16[4,2,640,128]{3,2,1,0:T(8,128)(2,1)}, bf16[4,2,640,128]{3,2,1,0:T(8,128)(2,1)S(1)}, u32[]{:S(2)}, u32[]{:S(2)}) collective-permute-start(bf16[4,2,640,128]{3,2,1,0:T(8,128)(2,1)} %get-tuple-element.9), channel_id=1, source_target_pairs={{0,32},{32,0},{64,96},{96,64},{128,160},{160,128},{192,224},{224,1... | collective-permute-start | bytes 3932168 | tf_op jit(solution)/shard_map/ppermute | solution.py:296
  13.8 2.7 %copy-start.5 = (bf16[4,2,640,128]{3,2,1,0:T(8,128)(2,1)S(1)}, bf16[4,2,640,128]{3,2,1,0:T(8,128)(2,1)}, u32[]{:S(2)}) copy-start(bf16[4,2,640,128]{3,2,1,0:T(8,128)(2,1)} %get-tuple-element.8.refs_0_) | copy-start | bytes 3932164
  13.9 18.9 %copy-start.3 = (bf16[4,2,640,128]{3,2,1,0:T(8,128)(2,1)}, bf16[4,2,640,128]{3,2,1,0:T(8,128)(2,1)S(1)}, u32[]{:S(2)}) copy-start(bf16[4,2,640,128]{3,2,1,0:T(8,128)(2,1)S(1)} %collective-permute-done.3.refs_5_) | copy-start | bytes 3932164
  15.6 17.1 %collective-permute-start.4 = (bf16[2,2,640,128]{3,2,1,0:T(8,128)(2,1)S(1)}, bf16[2,2,640,128]{3,2,1,0:T(8,128)(2,1)S(1)}, u32[]{:S(2)}, u32[]{:S(2)}) collective-permute-start(bf16[2,2,640,128]{3,2,1,0:T(8,128)(2,1)S(1)} %add_convert_fusion), channel_id=1, source_target_pairs={{0,192},{32,224},{64,128},{96,160},{128,64},{160,96},{192,0},{224,... | collective-permute-start | bytes 1966088 | tf_op jit(solution)/shard_map/ppermute | solution.py:296
  16.5 17.6 %copy-start.4 = (bf16[4,2,640,128]{3,2,1,0:T(8,128)(2,1)}, bf16[4,2,640,128]{3,2,1,0:T(8,128)(2,1)S(1)}, u32[]{:S(2)}) copy-start(bf16[4,2,640,128]{3,2,1,0:T(8,128)(2,1)S(1)} %collective-permute-done.refs_1_) | copy-start | bytes 3932164
  16.7 17.4 %collective-permute-start.1 = (bf16[2,2,640,128]{3,2,1,0:T(8,128)(2,1)S(1)}, bf16[2,2,640,128]{3,2,1,0:T(8,128)(2,1)S(1)}, u32[]{:S(2)}, u32[]{:S(2)}) collective-permute-start(bf16[2,2,640,128]{3,2,1,0:T(8,128)(2,1)S(1)} %add_convert_fusion.1), channel_id=1, source_target_pairs={{0,64},{32,96},{64,0},{96,32},{128,192},{160,224},{192,128},{224,1... | collective-permute-start | bytes 1966088 | tf_op jit(solution)/shard_map/ppermute | solution.py:296
  32.7 1.6 copy-start.6
  34.0 8.0 %collective-permute-start.5 = (bf16[1,2,640,128]{3,2,1,0:T(8,128)(2,1)S(1)}, bf16[1,2,640,128]{3,2,1,0:T(8,128)(2,1)S(1)}, u32[]{:S(2)}, u32[]{:S(2)}) collective-permute-start(bf16[1,2,640,128]{3,2,1,0:T(8,128)(2,1)S(1)} %add_convert_fusion.2), channel_id=1, source_target_pairs={{0,64},{32,96},{64,0},{96,32},{128,192},{160,224},{192,128},{224,1... | collective-permute-start | bytes 983048 | tf_op jit(solution)/shard_map/ppermute | solution.py:296
  34.1 7.9 %copy-start.7 = (bf16[2,2,640,128]{3,2,1,0:T(8,128)(2,1)}, bf16[2,2,640,128]{3,2,1,0:T(8,128)(2,1)S(1)}, u32[]{:S(2)}) copy-start(bf16[2,2,640,128]{3,2,1,0:T(8,128)(2,1)S(1)} %collective-permute-done.1.refs_2_) | copy-start | bytes 1966084
  34.3 9.2 %collective-permute-start.2 = (bf16[1,2,640,128]{3,2,1,0:T(8,128)(2,1)S(1)}, bf16[1,2,640,128]{3,2,1,0:T(8,128)(2,1)S(1)}, u32[]{:S(2)}, u32[]{:S(2)}) collective-permute-start(bf16[1,2,640,128]{3,2,1,0:T(8,128)(2,1)S(1)} %add_convert_fusion.3), channel_id=1, source_target_pairs={{0,192},{32,224},{64,128},{96,160},{128,64},{160,96},{192,0},{224,... | collective-permute-start | bytes 983048 | tf_op jit(solution)/shard_map/ppermute | solution.py:296
  42.0 1.5 copy-start.9
  43.5 0.7 copy-start.10
  53.2 5.8 %copy-start.8 = (s32[512]{0:T(512)S(1)}, s32[512]{0:T(512)}, u32[]{:S(2)}) copy-start(s32[512]{0:T(512)} %param.3) | copy-start | bytes 6148
  53.2 16.6 %all-to-all-start = ((bf16[8,2,160,128]{3,2,1,0:T(8,128)(2,1)}), bf16[8,2,160,128]{3,2,1,0:T(8,128)(2,1)S(1)}, u32[]{:S(2)}, u32[]{:S(2)}) async-start(bf16[8,2,160,128]{3,2,1,0:T(8,128)(2,1)} %get-tuple-element.12), calls=%async_computation | async-start | bytes 1310720 | tf_op jit(solution)/shard_map/all_to_all | solution.py:332
  69.8 0.8 copy-start.2
  73.0 41.5 %all-to-all-start.1 = ((bf16[32,160,128]{2,1,0:T(8,128)(2,1)}), bf16[32,160,128]{2,1,0:T(8,128)(2,1)S(1)}, u32[]{:S(2)}, u32[]{:S(2)}) async-start(bf16[32,160,128]{2,1,0:T(8,128)(2,1)} %send_pick.1), calls=%async_computation.1 | async-start | bytes 2621440 | tf_op jit(solution)/shard_map/all_to_all | solution.py:335
  114.5 9.4 %copy-start = (bf16[32,160,128]{2,1,0:T(8,128)(2,1)}, bf16[32,160,128]{2,1,0:T(8,128)(2,1)S(1)}, u32[]{:S(2)}) copy-start(bf16[32,160,128]{2,1,0:T(8,128)(2,1)S(1)} %all-to-all-done.1.source_ref) | copy-start | bytes 3932164
  114.5 22.1 %all-to-all-start.3 = ((bf16[8,2,64,512]{3,2,1,0:T(8,128)(2,1)}), bf16[8,2,64,512]{3,2,1,0:T(8,128)(2,1)S(1)}, u32[]{:S(2)}, u32[]{:S(2)}) async-start(bf16[8,2,64,512]{3,2,1,0:T(8,128)(2,1)} %get-tuple-element.13), calls=%async_computation.3 | async-start | bytes 2097152 | tf_op jit(solution)/shard_map/all_to_all | solution.py:333
  136.6 18.7 %all-to-all-start.2 = ((bf16[24,160,128]{2,1,0:T(8,128)(2,1)}), bf16[24,160,128]{2,1,0:T(8,128)(2,1)S(1)}, u32[]{:S(2)}, u32[]{:S(2)}) async-start(bf16[24,160,128]{2,1,0:T(8,128)(2,1)} %slot_pick.1), calls=%async_computation.2 | async-start | bytes 1966080 | tf_op jit(solution)/shard_map/all_to_all | solution.py:338
  155.3 0.9 copy-start.1
